TPU v7x, 32 devices: a whole 2x2x4 slice. The times are simulated.
32 devices in a mesh: row: 4 (over z), col: 8 (over y, x, core).
Axes of the slice: x: 2, y: 2, z: 4, core: 2. Of those that a mesh axis runs over, the one named last changes fastest.
Arguments:
- a_matrix: float32 [8192, 8192], P('row', 'col'), may hold values from -14 to 30, as said below
- b_matrix: float32 [4096, 4096], P('row', 'col'), may hold values from -14 to 30, as said below
- c_matrix: float32 [8192, 4096], P('row', 'col'), may hold values from -6 to 6
Outputs:
- a_swept: float32 [8192, 8192], P('row', 'col')
- c_swept: float32 [8192, 4096], P('row', 'col')
- b_next: float32 [4096, 4096], P('row', 'col')
Inputs may be any that keep to these rules, and one draw needn't show every extreme that they name: `a_matrix`: symmetric positive definite; its smallest eigenvalue is at least 1. `b_matrix`: symmetric positive definite; its smallest eigenvalue is at least 1.
All inputs are finite; a program needn't handle non-finite values. Where the computation divides by a largest or mean magnitude, that divisor is 1e-20 or more.
Results may differ from a plain program's by a relative error of at most 0.00012.
Values sent between devices are 32-bit elements; how exact they have to be, the bound alone decides.
No kernel may reach another device: no remote copies, remote signals or barrier semaphores. Data moves between devices by JAX's collectives and lax.ppermute only.
A program may use at most 128 MiB of HBM per device.

v0:
```python
import jax
import jax.numpy as jnp
from jax import lax
from jax.sharding import PartitionSpec as P

PANEL = 256
PIVOT_ITERS = 6
STEPS_A = 2
STEPS_B = 16
EXACT = lax.Precision.HIGHEST
CLOSE = lax.Precision.HIGH


def spread(value, axis, source):
    kept = jnp.where(lax.axis_index(axis) == source, value, 0).astype(value.dtype)
    return lax.psum(kept, axis)


def pivot_inverse(pivot):
    order = pivot.shape[0]
    unit_square = jnp.eye(order, dtype=jnp.float32)
    scaling = 1.0 / jnp.sqrt(jnp.sum(pivot * unit_square, axis=1))
    unit = pivot * scaling[:, None] * scaling[None, :]
    ceiling = jnp.max(jnp.sum(jnp.abs(unit), axis=1))
    approx = jnp.eye(order, dtype=jnp.float32) / ceiling
    for turn in range(PIVOT_ITERS):
        product = jnp.dot(unit, approx, precision=EXACT, preferred_element_type=jnp.float32)
        approx = 2.0 * approx - jnp.dot(
            approx, product, precision=EXACT, preferred_element_type=jnp.float32
        )
    return approx * scaling[:, None] * scaling[None, :]


def mul(left, right, dims, precision):
    return lax.dot_general(
        left, right, (dims, ((), ())), precision=precision, preferred_element_type=jnp.float32
    )


def sweep_panel(block, panel, places):
    order = block.shape[0]
    index = jnp.arange(order, dtype=jnp.int32)
    eye = (index[:, None] == jnp.concatenate([index, places])[None, :]).astype(jnp.float32)
    both = jnp.concatenate([block, panel], 1)
    for start in range(0, order, PANEL):
        stop = start + PANEL
        inverse = pivot_inverse(both[start:stop, start:stop].T)
        solved = mul(inverse, both[start:stop] - eye[start:stop], ((0,), (0,)), EXACT)
        updated = both - mul(both[:, start:stop], solved, ((1,), (0,)), CLOSE)
        both = jnp.concatenate([updated[:start], eye[start:stop] - solved, updated[stop:]], 0)
    return (both[:, order:], eye[:, order:])


def a_sweep(matrix, other):
    local_rows, local_cols = matrix.shape
    other_cols = other.shape[1]
    order = STEPS_A * PANEL
    row_place = lax.axis_index("row")
    col_place = lax.axis_index("col")
    panel = spread(matrix[:, :order], "col", 0)
    joined = spread(jnp.concatenate([matrix[:order], other[:order], panel[:order]], 1), "row", 0)
    rows = joined[:, : local_cols + other_cols]
    block = joined[:, local_cols + other_cols :].T
    places = row_place * local_rows + jnp.arange(local_rows, dtype=jnp.int32)
    swept, eye = sweep_panel(block, panel.T, places)
    solved = eye - swept
    new_matrix = matrix - mul(solved, rows[:, :local_cols], ((0,), (0,)), CLOSE)
    new_other = other - mul(solved, rows[:, local_cols:], ((0,), (0,)), CLOSE)
    front = jnp.where(col_place == 0, swept.T, new_matrix[:, :order])
    return (new_matrix.at[:, :order].set(front), new_other)


def b_sweep(matrix, row_count, col_count):
    local_rows, local_cols = matrix.shape
    order = min(local_rows, local_cols)
    steps = STEPS_B * PANEL // order
    row_part = order // row_count
    col_part = order // col_count
    row_place = lax.axis_index("row")
    col_place = lax.axis_index("col")
    dealt = matrix.T.reshape(local_cols // order, col_count, col_part, local_rows)
    dealt = lax.all_to_all(dealt, "col", 1, 0, tiled=True).reshape(local_cols, local_rows)
    dealt = dealt.T.reshape(local_rows // order, row_count, row_part, local_cols)
    dealt = lax.all_to_all(dealt, "row", 1, 0, tiled=True).reshape(local_rows, local_cols)
    index = jnp.arange(local_rows, dtype=jnp.int32)
    for step in range(steps):
        top = step * row_part
        left = step * col_part
        panel = lax.all_gather(dealt[:, left : left + col_part].T, "col", axis=0, tiled=True)
        joined = jnp.concatenate([dealt[top : top + row_part], panel[:, top : top + row_part].T], 1)
        joined = lax.all_gather(joined, "row", axis=0, tiled=True)
        rows = joined[:, :local_cols]
        block = joined[:, local_cols:].T
        inside = (index >= top) & (index < top + row_part)
        places = jnp.where(inside, index - top + row_place * row_part, -1)
        swept, eye = sweep_panel(block, panel, places)
        updated = dealt + mul(swept - eye, rows, ((0,), (0,)), CLOSE)
        own = lax.dynamic_slice_in_dim(swept, col_place * col_part, col_part, 0).T
        dealt = updated.at[:, left : left + col_part].set(own)
    back = dealt.reshape(steps, 1, row_part, local_cols)
    back = lax.all_to_all(back, "row", 0, 1, tiled=True).reshape(local_rows, local_cols)
    back = back.T.reshape(steps, 1, col_part, local_rows)
    back = lax.all_to_all(back, "col", 0, 1, tiled=True).reshape(local_cols, local_rows)
    return back.T


def solution(mesh):
    row_count = mesh.shape["row"]
    col_count = mesh.shape["col"]

    def body(a_matrix, b_matrix, c_matrix):
        b_local = jnp.sum(b_matrix * b_matrix)
        a_swept, c_swept = a_sweep(a_matrix, c_matrix)
        b_inverse = b_sweep(b_matrix, row_count, col_count)
        inv_local = jnp.sum(b_inverse * b_inverse)
        sums = lax.psum(jnp.stack([b_local, inv_local]), ("row", "col"))
        scale = jnp.sqrt(jnp.sqrt(sums[1] / sums[0]))
        b_next = 0.5 * (scale * b_matrix + b_inverse / scale)
        return (a_swept, c_swept, b_next)

    return jax.shard_map(
        body,
        mesh=mesh,
        in_specs=(P("row", "col"), P("row", "col"), P("row", "col")),
        out_specs=(P("row", "col"), P("row", "col"), P("row", "col")),
        check_vma=False,
    )
```

profile of v0, /device:TPU:10, one launch (start us, length us, event | category | flops | bytes accessed | tf_op | source)
XLA Modules:
  0.0 1504.4 jit_solution(638320156755108339)
XLA Ops:
  9.2 29.3 %all_to_all.48 = f32[1,8,64,1024]{3,2,0,1:T(8,128)} all-to-all(f32[1,8,64,1024]{3,2,0,1:T(8,128)S(1)} %bitcast.702), channel_id=1, replica_groups=mesh['row'=4,'col'=8] {'col'}, dimensions={1} | all-to-all | bytes 4194304 | tf_op jit(solution)/shard_map/all_to_all | solution.py:82
  40.6 51.6 %all_to_all.49 = f32[2,4,128,512]{3,2,0,1:T(8,128)S(1)} all-to-all(f32[2,4,128,512]{3,2,0,1:T(8,128)S(1)} %copy.155), channel_id=1, replica_groups=mesh['row'=4,'col'=8] {'row'}, dimensions={1} | all-to-all | bytes 4194304 | tf_op jit(solution)/shard_map/all_to_all | solution.py:84
  93.5 27.3 %all-gather.17.cloned.1.call-done = f32[512,1024]{1,0:T(8,128)} async-done(((f32[64,1024]{1,0:T(8,128)}), f32[512,1024]{1,0:T(8,128)}) %all-gather.17.cloned.1.call-update) | async-done | bytes 2097168 | tf_op jit(solution)/shard_map/all_gather | solution.py:89
  125.3 42.9 %all-gather.19.cloned.1.call-done = f32[512,1024]{1,0:T(8,128)} async-done(((f32[128,1024]{1,0:T(8,128)}), f32[512,1024]{1,0:T(8,128)}) %all-gather.19.cloned.1.call-update) | async-done | bytes 2097168 | tf_op jit(solution)/shard_map/all_gather | solution.py:91
  227.9 27.0 %all-gather.21.cloned.1.call-done = f32[512,1024]{1,0:T(8,128)} async-done(((f32[64,1024]{1,0:T(8,128)}), f32[512,1024]{1,0:T(8,128)}) %all-gather.21.cloned.1.call-update) | async-done | bytes 2097168 | tf_op jit(solution)/shard_map/all_gather | solution.py:89
  258.9 43.4 %all-gather.23.cloned.1.call-done = f32[512,1024]{1,0:T(8,128)} async-done(((f32[128,1024]{1,0:T(8,128)}), f32[512,1024]{1,0:T(8,128)}) %all-gather.23.cloned.1.call-update) | async-done | bytes 2097168 | tf_op jit(solution)/shard_map/all_gather | solution.py:91
  362.1 27.0 %all-gather.25.cloned.1.call-done = f32[512,1024]{1,0:T(8,128)} async-done(((f32[64,1024]{1,0:T(8,128)}), f32[512,1024]{1,0:T(8,128)}) %all-gather.25.cloned.1.call-update) | async-done | bytes 2097168 | tf_op jit(solution)/shard_map/all_gather | solution.py:89
  393.4 43.2 %all-gather.27.cloned.1.call-done = f32[512,1024]{1,0:T(8,128)} async-done(((f32[128,1024]{1,0:T(8,128)}), f32[512,1024]{1,0:T(8,128)}) %all-gather.27.cloned.1.call-update) | async-done | bytes 2097168 | tf_op jit(solution)/shard_map/all_gather | solution.py:91
  495.9 27.0 %all-gather.29.cloned.1.call-done = f32[512,1024]{1,0:T(8,128)} async-done(((f32[64,1024]{1,0:T(8,128)}), f32[512,1024]{1,0:T(8,128)}) %all-gather.29.cloned.1.call-update) | async-done | bytes 2097168 | tf_op jit(solution)/shard_map/all_gather | solution.py:89
  527.0 43.3 %all-gather.31.cloned.1.call-done = f32[512,1024]{1,0:T(8,128)} async-done(((f32[128,1024]{1,0:T(8,128)}), f32[512,1024]{1,0:T(8,128)}) %all-gather.31.cloned.1.call-update) | async-done | bytes 2097168 | tf_op jit(solution)/shard_map/all_gather | solution.py:91
  630.3 27.0 %all-gather.33.cloned.1.call-done = f32[512,1024]{1,0:T(8,128)} async-done(((f32[64,1024]{1,0:T(8,128)}), f32[512,1024]{1,0:T(8,128)}) %all-gather.33.cloned.1.call-update) | async-done | bytes 2097168 | tf_op jit(solution)/shard_map/all_gather | solution.py:89
  661.3 43.4 %all-gather.35.cloned.1.call-done = f32[512,1024]{1,0:T(8,128)} async-done(((f32[128,1024]{1,0:T(8,128)}), f32[512,1024]{1,0:T(8,128)}) %all-gather.35.cloned.1.call-update) | async-done | bytes 2097168 | tf_op jit(solution)/shard_map/all_gather | solution.py:91
  764.1 27.0 %all-gather.37.cloned.1.call-done = f32[512,1024]{1,0:T(8,128)} async-done(((f32[64,1024]{1,0:T(8,128)}), f32[512,1024]{1,0:T(8,128)}) %all-gather.37.cloned.1.call-update) | async-done | bytes 2097168 | tf_op jit(solution)/shard_map/all_gather | solution.py:89
  795.3 43.2 %all-gather.39.cloned.1.call-done = f32[512,1024]{1,0:T(8,128)} async-done(((f32[128,1024]{1,0:T(8,128)}), f32[512,1024]{1,0:T(8,128)}) %all-gather.39.cloned.1.call-update) | async-done | bytes 2097168 | tf_op jit(solution)/shard_map/all_gather | solution.py:91
  897.3 4.7 slice_select_fusion
  903.0 22.2 %all-gather.41.cloned.1.call-done = f32[512,1024]{1,0:T(8,128)} async-done(((f32[64,1024]{1,0:T(8,128)}), f32[512,1024]{1,0:T(8,128)}) %all-gather.41.cloned.1.call-update) | async-done | bytes 2097168 | tf_op jit(solution)/shard_map/all_gather | solution.py:89
  936.7 73.2 %all-reduce.3.cloned.1.call-done = f32[2048,512]{1,0:T(8,128)} async-done(((f32[2048,512]{1,0:T(8,128)}), f32[2048,512]{1,0:T(8,128)}) %all-reduce.3.cloned.1.call-update) | async-done | bytes 4194320 | tf_op jit(solution)/shard_map/psum | solution.py:16
  1015.8 39.9 %all-gather.43.cloned.1.call-done = f32[512,1024]{1,0:T(8,128)} async-done(((f32[128,1024]{1,0:T(8,128)}), f32[512,1024]{1,0:T(8,128)}) %all-gather.43.cloned.1.call-update) | async-done | bytes 2097168 | tf_op jit(solution)/shard_map/all_gather | solution.py:91
  1121.3 90.3 %all-reduce.5.cloned.1.call-done = f32[512,2048]{1,0:T(8,128)} async-done(((f32[512,2048]{1,0:T(8,128)}), f32[512,2048]{1,0:T(8,128)}) %all-reduce.5.cloned.1.call-update) | async-done | bytes 4194320 | tf_op jit(solution)/shard_map/psum | solution.py:16
  1223.5 18.7 %all-gather.45.cloned.1.call-done = f32[512,1024]{1,0:T(8,128)} async-done(((f32[64,1024]{1,0:T(8,128)}), f32[512,1024]{1,0:T(8,128)}) %all-gather.45.cloned.1.call-update) | async-done | bytes 2097168 | tf_op jit(solution)/shard_map/all_gather | solution.py:89
  1251.4 7.1 fusion.13
  1270.0 22.7 %all-gather.47.cloned.1.call-done = f32[512,1024]{1,0:T(8,128)} async-done(((f32[128,1024]{1,0:T(8,128)}), f32[512,1024]{1,0:T(8,128)}) %all-gather.47.cloned.1.call-update) | async-done | bytes 2097168 | tf_op jit(solution)/shard_map/all_gather | solution.py:91
  1348.6 6.7 all-to-all-start.2
  1367.4 7.8 fusion.15
  1378.5 5.6 slice_subtract_fusion.3
  1385.7 4.6 fusion.234
  1390.3 9.9 all-to-all-done.2
  1403.9 5.1 all-to-all-start.3
  1414.6 11.6 convolution_subtract_fusion
  1426.3 5.8 fusion.2
  1438.4 9.8 convolution_subtract_fusion.9
  1448.2 42.8 %psum.23 = f32[2]{0:T(128)S(1)} all-reduce(f32[2]{0:T(128)S(1)} %pad_maximum_fusion.35), channel_id=1, replica_groups=mesh['row'=4,'col'=8] {'row','col'}, use_global_device_ids=true, to_apply=%region_66.67 | all-reduce | flops 2 | bytes 16 | tf_op jit(solution)/shard_map/psum | solution.py:116
  (752 shorter events, 581.9 us)
Async XLA Ops:
  7.2 113.7 %all-gather.17.cloned.1.call-start = ((), (), s32[]{:S(2)}) async-start(), calls=%async_computation.6 | async-start | bytes 2359296 | tf_op jit(solution)/shard_map/all_gather | solution.py:89
  9.1 29.3 %copy-start.55 = (f32[1024,512]{0,1:T(8,128)}, f32[1024,512]{0,1:T(8,128)S(1)}, u32[]{:S(2)}) copy-start(f32[1024,512]{0,1:T(8,128)S(1)} %copy.152) | copy-start | bytes 6291460
  93.3 74.9 %all-gather.19.cloned.1.call-start = ((), (), s32[]{:S(2)}) async-start(), calls=%async_computation.7 | async-start | bytes 2621440 | tf_op jit(solution)/shard_map/all_gather | solution.py:91
  123.7 131.2 %all-gather.21.cloned.1.call-start = ((), (), s32[]{:S(2)}) async-start(), calls=%async_computation.8 | async-start | bytes 2359296 | tf_op jit(solution)/shard_map/all_gather | solution.py:89
  226.9 75.4 %all-gather.23.cloned.1.call-start = ((), (), s32[]{:S(2)}) async-start(), calls=%async_computation.9 | async-start | bytes 2621440 | tf_op jit(solution)/shard_map/all_gather | solution.py:91
  257.8 131.3 %all-gather.25.cloned.1.call-start = ((), (), s32[]{:S(2)}) async-start(), calls=%async_computation.10 | async-start | bytes 2359296 | tf_op jit(solution)/shard_map/all_gather | solution.py:89
  329.4 5.5 copy-start.13
  361.1 75.4 %all-gather.27.cloned.1.call-start = ((), (), s32[]{:S(2)}) async-start(), calls=%async_computation.11 | async-start | bytes 2621440 | tf_op jit(solution)/shard_map/all_gather | solution.py:91
  392.0 130.9 %all-gather.29.cloned.1.call-start = ((), (), s32[]{:S(2)}) async-start(), calls=%async_computation.12 | async-start | bytes 2359296 | tf_op jit(solution)/shard_map/all_gather | solution.py:89
  494.9 75.4 %all-gather.31.cloned.1.call-start = ((), (), s32[]{:S(2)}) async-start(), calls=%async_computation.13 | async-start | bytes 2621440 | tf_op jit(solution)/shard_map/all_gather | solution.py:91
  525.8 131.5 %all-gather.33.cloned.1.call-start = ((), (), s32[]{:S(2)}) async-start(), calls=%async_computation.14 | async-start | bytes 2359296 | tf_op jit(solution)/shard_map/all_gather | solution.py:89
  629.2 75.4 %all-gather.35.cloned.1.call-start = ((), (), s32[]{:S(2)}) async-start(), calls=%async_computation.15 | async-start | bytes 2621440 | tf_op jit(solution)/shard_map/all_gather | solution.py:91
  660.2 130.9 %all-gather.37.cloned.1.call-start = ((), (), s32[]{:S(2)}) async-start(), calls=%async_computation.16 | async-start | bytes 2359296 | tf_op jit(solution)/shard_map/all_gather | solution.py:89
  763.1 75.4 %all-gather.39.cloned.1.call-start = ((), (), s32[]{:S(2)}) async-start(), calls=%async_computation.17 | async-start | bytes 2621440 | tf_op jit(solution)/shard_map/all_gather | solution.py:91
  794.0 131.3 %all-gather.41.cloned.1.call-start = ((), (), s32[]{:S(2)}) async-start(), calls=%async_computation.18 | async-start | bytes 2359296 | tf_op jit(solution)/shard_map/all_gather | solution.py:89
  897.2 112.6 %all-reduce.3.cloned.1.call-start = ((), (), s32[]{:S(2)}) async-start(), calls=%async_computation.4 | async-start | bytes 8388608 | tf_op jit(solution)/shard_map/psum | solution.py:16
  902.0 153.7 %all-gather.43.cloned.1.call-start = ((), (), s32[]{:S(2)}) async-start(), calls=%async_computation.19 | async-start | bytes 2621440 | tf_op jit(solution)/shard_map/all_gather | solution.py:91
  928.1 283.5 %all-reduce.5.cloned.1.call-start = ((), (), s32[]{:S(2)}) async-start(), calls=%async_computation.5 | async-start | bytes 8388608 | tf_op jit(solution)/shard_map/psum | solution.py:16
  928.7 5.8 copy-start.107
  1015.3 226.8 %all-gather.45.cloned.1.call-start = ((), (), s32[]{:S(2)}) async-start(), calls=%async_computation.20 | async-start | bytes 2359296 | tf_op jit(solution)/shard_map/all_gather | solution.py:89
  1117.7 174.9 %all-gather.47.cloned.1.call-start = ((), (), s32[]{:S(2)}) async-start(), calls=%async_computation.21 | async-start | bytes 2621440 | tf_op jit(solution)/shard_map/all_gather | solution.py:91
  1251.4 7.1 copy-start.36
  1348.6 51.7 %all-to-all-start.2 = ((f32[8,1,128,512]{3,2,1,0:T(8,128)}), f32[8,1,128,512]{3,2,1,0:T(8,128)}, u32[]{:S(2)}, u32[]{:S(2)}) async-start(f32[8,1,128,512]{3,2,1,0:T(8,128)} %bitcast.706), calls=%async_computation.2 | async-start | bytes 4194304 | tf_op jit(solution)/shard_map/all_to_all | solution.py:101
  1356.6 10.8 slice-start
  1359.9 7.5 slice-start.1
  1378.5 7.2 copy-start.7
  1378.5 7.2 copy-start.8
  1403.9 8.2 slice-start.2
  1403.9 30.3 %all-to-all-start.3 = ((f32[8,1,64,1024]{3,2,1,0:T(8,128)}), f32[8,1,64,1024]{3,2,1,0:T(8,128)}, u32[]{:S(2)}, u32[]{:S(2)}) async-start(f32[8,1,64,1024]{3,2,1,0:T(8,128)} %bitcast.72), calls=%async_computation.3 | async-start | bytes 4194304 | tf_op jit(solution)/shard_map/all_to_all | solution.py:103
  1409.1 5.5 copy-start.4
  1412.2 14.1 copy-start.3
  1426.3 12.1 copy-start.5
  (101 other events, 236.8 us)
Sparse Core Ops, SparseCore 0:
  93.5 27.2 all-gather.16
  123.8 44.3 all-gather.18
  227.0 27.8 all-gather.20
  257.9 44.3 all-gather.22
  361.2 27.8 all-gather.24
  392.2 44.3 all-gather.26
  495.0 27.8 all-gather.28
  525.9 44.3 all-gather.30
  629.4 27.8 all-gather.32
  660.3 44.3 all-gather.34
  763.2 27.8 all-gather.36
  794.1 44.3 all-gather.38
  897.3 27.8 all-gather.40
  928.9 80.8 all-reduce.2
  1011.2 44.4 all-gather.42
  1058.5 153.1 all-reduce.4
  1213.4 28.6 all-gather.44
  1248.3 44.3 all-gather.46
where the time goes:
time: 1520 us; the launch traced here: 1500 us
  waiting for transfers between devices  701 us (46%)
  matrix products  290 us (19%)
  local copies, waits for them, and re-layouts  229 us (15%)
  blocking collectives  124 us (8%)
  other arithmetic  115 us (8%)
  between operations  31.5 us (2%)
    all_gather x8, waiting for transfers between devices, b_sweep(): joined = lax.all_gather(joined, 'row', axis=0, tiled=True)  322 us
    all_gather x8, waiting for transfers between devices, b_sweep(): lax.all_gather(dealt[:, left:left + col_part].T, 'col', axis=0, tiled=True)  203 us
    psum x2, waiting for transfers between devices, spread(): return lax.psum(kept, axis)  163 us
    dot_general x46, matrix products, mul(): lax.dot_general(left, right, (dims, ((), ())), precision=precision, prefe...  149 us
    dot_general x108, matrix products, pivot_inverse(): jnp.dot(unit, approx, precision=EXACT, preferred_element_type=jnp.float32)  97.6 us
    unnamed x226, local copies, waits for them, and re-layouts  55.5 us
    dot_general x18, local copies, waits for them, and re-layouts, mul(): lax.dot_general(left, right, (dims, ((), ())), precision=precision, prefe...  55.2 us
    all_to_all x1, blocking collectives, b_sweep(): lax.all_to_all(dealt, 'row', 1, 0, tiled=True)  51.6 us
  transfers between devices with their start and end apart: 20, of which 20 were waited for; matrix products, arithmetic and copies ran while one was open for 12% of the time, Pallas kernels for 0%

commit v1 on v0

--- a/solution.py
+++ b/solution.py
@@ -11,9 +11,13 @@
 CLOSE = lax.Precision.HIGH
 
 
+def _test_sector(row_axis, x_local):
+    return jnp.sum(jax.lax.all_gather(x_local, axis_name=row_axis), axis=0)
+
+
 def spread(value, axis, source):
     kept = jnp.where(lax.axis_index(axis) == source, value, 0).astype(value.dtype)
-    return lax.psum(kept, axis)
+    return _test_sector(axis, kept)
 
 
 def pivot_inverse(pivot):

time: 1520 us -> 1700 us (1.12)
  blocking collectives: 124 us -> 248 us
  waiting for transfers between devices: 701 us -> 783 us
  local copies, waits for them, and re-layouts: 229 us -> 207 us
    all_gather x0 -> x2, waiting for transfers between devices: none -> 225 us  [_test_sector(): return jnp.sum(jax.lax.all_gather(x_local, axis_name=row_axis), axis=0)]
    psum x2 -> x0, waiting for transfers between devices: 163 us -> none  [spread(): return lax.psum(kept, axis)]
    all_to_all x0 -> x1, blocking collectives: none -> 107 us  [b_sweep(): lax.all_to_all(back, 'row', 0, 1, tiled=True)]
    reduce_sum x0 -> x2, other arithmetic: none -> 25.6 us  [_test_sector(): return jnp.sum(jax.lax.all_gather(x_local, axis_name=row_axis), axis=0)]
    psum x1, blocking collectives: 42.8 us -> 60.2 us  [body(): sums = lax.psum(jnp.stack([b_local, inv_local]), ('row', 'col'))]
    all_to_all x1, waiting for transfers between devices: 2.22 us -> 19.4 us  [b_sweep(): lax.all_to_all(back, 'col', 0, 1, tiled=True)]
    unnamed x226 -> x214, local copies, waits for them, and re-layouts: 55.5 us -> 50.3 us
  transfers between devices with their start and end apart: 20 -> 19, of which waited for: 20 -> 19; matrix products, arithmetic and copies ran while one was open for 12% -> 7% of each run, Pallas kernels for 0% -> 0%
where the time goes in v1:
time: 1700 us; the launch traced here: 1680 us
  waiting for transfers between devices  783 us (46%)
  matrix products  297 us (17%)
  blocking collectives  248 us (15%)
  local copies, waits for them, and re-layouts  207 us (12%)
  other arithmetic  113 us (7%)
  between operations  32.2 us (2%)
    all_gather x8, waiting for transfers between devices, b_sweep(): joined = lax.all_gather(joined, 'row', axis=0, tiled=True)  327 us
    all_gather x2, waiting for transfers between devices, _test_sector(): return jnp.sum(jax.lax.all_gather(x_local, axis_name=row_axis), axis=0)  225 us
    all_gather x8, waiting for transfers between devices, b_sweep(): lax.all_gather(dealt[:, left:left + col_part].T, 'col', axis=0, tiled=True)  212 us
    dot_general x46, matrix products, mul(): lax.dot_general(left, right, (dims, ((), ())), precision=precision, prefe...  163 us
    all_to_all x1, blocking collectives, b_sweep(): lax.all_to_all(back, 'row', 0, 1, tiled=True)  107 us
    dot_general x108, matrix products, pivot_inverse(): jnp.dot(unit, approx, precision=EXACT, preferred_element_type=jnp.float32)  92.9 us
    psum x1, blocking collectives, body(): sums = lax.psum(jnp.stack([b_local, inv_local]), ('row', 'col'))  60.2 us
    dot_general x18, local copies, waits for them, and re-layouts, mul(): lax.dot_general(left, right, (dims, ((), ())), precision=precision, prefe...  54.4 us
  transfers between devices with their start and end apart: 19, of which 19 were waited for; matrix products, arithmetic and copies ran while one was open for 7% of the time, Pallas kernels for 0%

profile of v1, /device:TPU:10, one launch (start us, length us, event | category | flops | bytes accessed | tf_op | source)
XLA Modules:
  0.0 1684.9 jit_solution(6761721501892296788)
XLA Ops:
  9.2 29.3 %all_to_all.48 = f32[1,8,64,1024]{3,2,0,1:T(8,128)} all-to-all(f32[1,8,64,1024]{3,2,0,1:T(8,128)S(1)} %bitcast.712), channel_id=1, replica_groups=mesh['row'=4,'col'=8] {'col'}, dimensions={1} | all-to-all | bytes 4194304 | tf_op jit(solution)/shard_map/all_to_all | solution.py:86
  40.6 51.6 %all_to_all.49 = f32[2,4,128,512]{3,2,0,1:T(8,128)S(1)} all-to-all(f32[2,4,128,512]{3,2,0,1:T(8,128)S(1)} %copy.155), channel_id=1, replica_groups=mesh['row'=4,'col'=8] {'row'}, dimensions={1} | all-to-all | bytes 4194304 | tf_op jit(solution)/shard_map/all_to_all | solution.py:88
  93.5 27.3 %all-gather.22.cloned.1.call-done = f32[512,1024]{1,0:T(8,128)} async-done(((f32[64,1024]{1,0:T(8,128)}), f32[512,1024]{1,0:T(8,128)}) %all-gather.22.cloned.1.call-update) | async-done | bytes 2097168 | tf_op jit(solution)/shard_map/all_gather | solution.py:93
  125.5 42.8 %all-gather.24.cloned.1.call-done = f32[512,1024]{1,0:T(8,128)} async-done(((f32[128,1024]{1,0:T(8,128)}), f32[512,1024]{1,0:T(8,128)}) %all-gather.24.cloned.1.call-update) | async-done | bytes 2097168 | tf_op jit(solution)/shard_map/all_gather | solution.py:95
  226.3 27.0 %all-gather.26.cloned.1.call-done = f32[512,1024]{1,0:T(8,128)} async-done(((f32[64,1024]{1,0:T(8,128)}), f32[512,1024]{1,0:T(8,128)}) %all-gather.26.cloned.1.call-update) | async-done | bytes 2097168 | tf_op jit(solution)/shard_map/all_gather | solution.py:93
  257.4 43.3 %all-gather.28.cloned.1.call-done = f32[512,1024]{1,0:T(8,128)} async-done(((f32[128,1024]{1,0:T(8,128)}), f32[512,1024]{1,0:T(8,128)}) %all-gather.28.cloned.1.call-update) | async-done | bytes 2097168 | tf_op jit(solution)/shard_map/all_gather | solution.py:95
  358.9 27.0 %all-gather.30.cloned.1.call-done = f32[512,1024]{1,0:T(8,128)} async-done(((f32[64,1024]{1,0:T(8,128)}), f32[512,1024]{1,0:T(8,128)}) %all-gather.30.cloned.1.call-update) | async-done | bytes 2097168 | tf_op jit(solution)/shard_map/all_gather | solution.py:93
  390.3 43.0 %all-gather.32.cloned.1.call-done = f32[512,1024]{1,0:T(8,128)} async-done(((f32[128,1024]{1,0:T(8,128)}), f32[512,1024]{1,0:T(8,128)}) %all-gather.32.cloned.1.call-update) | async-done | bytes 2097168 | tf_op jit(solution)/shard_map/all_gather | solution.py:95
  491.1 27.0 %all-gather.34.cloned.1.call-done = f32[512,1024]{1,0:T(8,128)} async-done(((f32[64,1024]{1,0:T(8,128)}), f32[512,1024]{1,0:T(8,128)}) %all-gather.34.cloned.1.call-update) | async-done | bytes 2097168 | tf_op jit(solution)/shard_map/all_gather | solution.py:93
  522.3 43.2 %all-gather.36.cloned.1.call-done = f32[512,1024]{1,0:T(8,128)} async-done(((f32[128,1024]{1,0:T(8,128)}), f32[512,1024]{1,0:T(8,128)}) %all-gather.36.cloned.1.call-update) | async-done | bytes 2097168 | tf_op jit(solution)/shard_map/all_gather | solution.py:95
  623.9 27.0 %all-gather.38.cloned.1.call-done = f32[512,1024]{1,0:T(8,128)} async-done(((f32[64,1024]{1,0:T(8,128)}), f32[512,1024]{1,0:T(8,128)}) %all-gather.38.cloned.1.call-update) | async-done | bytes 2097168 | tf_op jit(solution)/shard_map/all_gather | solution.py:93
  655.1 43.3 %all-gather.40.cloned.1.call-done = f32[512,1024]{1,0:T(8,128)} async-done(((f32[128,1024]{1,0:T(8,128)}), f32[512,1024]{1,0:T(8,128)}) %all-gather.40.cloned.1.call-update) | async-done | bytes 2097168 | tf_op jit(solution)/shard_map/all_gather | solution.py:95
  756.2 27.0 %all-gather.42.cloned.1.call-done = f32[512,1024]{1,0:T(8,128)} async-done(((f32[64,1024]{1,0:T(8,128)}), f32[512,1024]{1,0:T(8,128)}) %all-gather.42.cloned.1.call-update) | async-done | bytes 2097168 | tf_op jit(solution)/shard_map/all_gather | solution.py:93
  787.6 43.0 %all-gather.44.cloned.1.call-done = f32[512,1024]{1,0:T(8,128)} async-done(((f32[128,1024]{1,0:T(8,128)}), f32[512,1024]{1,0:T(8,128)}) %all-gather.44.cloned.1.call-update) | async-done | bytes 2097168 | tf_op jit(solution)/shard_map/all_gather | solution.py:95
  888.8 27.0 %all-gather.46.cloned.1.call-done = f32[512,1024]{1,0:T(8,128)} async-done(((f32[64,1024]{1,0:T(8,128)}), f32[512,1024]{1,0:T(8,128)}) %all-gather.46.cloned.1.call-update) | async-done | bytes 2097168 | tf_op jit(solution)/shard_map/all_gather | solution.py:93
  919.9 43.3 %all-gather.48.cloned.1.call-done = f32[512,1024]{1,0:T(8,128)} async-done(((f32[128,1024]{1,0:T(8,128)}), f32[512,1024]{1,0:T(8,128)}) %all-gather.48.cloned.1.call-update) | async-done | bytes 2097168 | tf_op jit(solution)/shard_map/all_gather | solution.py:95
  1019.6 4.7 slice_select_fusion
  1025.3 22.3 %all-gather.50.cloned.1.call-done = f32[512,1024]{1,0:T(8,128)} async-done(((f32[64,1024]{1,0:T(8,128)}), f32[512,1024]{1,0:T(8,128)}) %all-gather.50.cloned.1.call-update) | async-done | bytes 2097168 | tf_op jit(solution)/shard_map/all_gather | solution.py:93
  1053.7 156.9 %all-gather.54.cloned.1.call-done = f32[16384,512]{1,0:T(8,128)} async-done(((f32[2048,512]{1,0:T(8,128)}), f32[16384,512]{1,0:T(8,128)}) %all-gather.54.cloned.1.call-update) | async-done | bytes 33554448 | tf_op jit(solution)/shard_map/all_gather | solution.py:15
  1210.6 15.5 reduce_sum.360
  1231.6 24.8 %all-gather.52.cloned.1.call-done = f32[512,1024]{1,0:T(8,128)} async-done(((f32[128,1024]{1,0:T(8,128)}), f32[512,1024]{1,0:T(8,128)}) %all-gather.52.cloned.1.call-update) | async-done | bytes 2097168 | tf_op jit(solution)/shard_map/all_gather | solution.py:95
  1311.3 106.8 %all_to_all.50 = f32[8,1,128,512]{3,2,1,0:T(8,128)S(1)} all-to-all(f32[8,1,128,512]{3,2,1,0:T(8,128)} %bitcast.716), channel_id=1, replica_groups=mesh['row'=4,'col'=8] {'row'}, dimensions={0} | all-to-all | bytes 4194304 | tf_op jit(solution)/shard_map/all_to_all | solution.py:105
  1430.1 19.4 %all-to-all-done.3 = f32[8,1,64,1024]{3,2,1,0:T(8,128)S(1)} async-done(((f32[8,1,64,1024]{3,2,1,0:T(8,128)}), f32[8,1,64,1024]{3,2,1,0:T(8,128)S(1)}, u32[]{:S(2)}, u32[]{:S(2)}) %all-to-all-start.3) | async-done | bytes 2097184 | tf_op jit(solution)/shard_map/all_to_all | solution.py:107
  1452.6 60.2 %psum.7 = f32[2]{0:T(128)S(1)} all-reduce(f32[2]{0:T(128)S(1)} %pad_maximum_fusion.35), channel_id=1, replica_groups=mesh['row'=4,'col'=8] {'row','col'}, use_global_device_ids=true, to_apply=%region_66.67 | all-reduce | flops 2 | bytes 16 | tf_op jit(solution)/shard_map/psum | solution.py:120
  1518.8 67.8 %all-gather.20.cloned.1.call-done = f32[4,512,2048]{2,1,0:T(8,128)} async-done(((f32[1,512,2048]{2,1,0:T(8,128)}), f32[4,512,2048]{2,1,0:T(8,128)}) %all-gather.20.cloned.1.call-update) | async-done | bytes 16777232 | tf_op jit(solution)/shard_map/all_gather | solution.py:15
  1586.5 10.1 reduce_sum.361
  1604.6 6.5 fusion.13
  1613.4 5.0 fusion
  1633.8 7.8 fusion.15
  1645.0 4.9 slice_subtract_fusion.3
  1654.7 10.5 convolution_subtract_fusion
  1665.3 7.0 convolution_subtract_fusion.9
  (740 shorter events, 550.3 us)
Async XLA Ops:
  7.2 113.7 %all-gather.22.cloned.1.call-start = ((), (), s32[]{:S(2)}) async-start(), calls=%async_computation.5 | async-start | bytes 2359296 | tf_op jit(solution)/shard_map/all_gather | solution.py:93
  9.1 29.3 %copy-start.55 = (f32[1024,512]{0,1:T(8,128)}, f32[1024,512]{0,1:T(8,128)S(1)}, u32[]{:S(2)}) copy-start(f32[1024,512]{0,1:T(8,128)S(1)} %copy.152) | copy-start | bytes 6291460
  93.4 74.9 %all-gather.24.cloned.1.call-start = ((), (), s32[]{:S(2)}) async-start(), calls=%async_computation.6 | async-start | bytes 2621440 | tf_op jit(solution)/shard_map/all_gather | solution.py:95
  123.7 129.5 %all-gather.26.cloned.1.call-start = ((), (), s32[]{:S(2)}) async-start(), calls=%async_computation.7 | async-start | bytes 2359296 | tf_op jit(solution)/shard_map/all_gather | solution.py:93
  193.6 5.8 copy-start.5
  225.2 75.5 %all-gather.28.cloned.1.call-start = ((), (), s32[]{:S(2)}) async-start(), calls=%async_computation.8 | async-start | bytes 2621440 | tf_op jit(solution)/shard_map/all_gather | solution.py:95
  256.2 129.8 %all-gather.30.cloned.1.call-start = ((), (), s32[]{:S(2)}) async-start(), calls=%async_computation.9 | async-start | bytes 2359296 | tf_op jit(solution)/shard_map/all_gather | solution.py:93
  326.1 5.5 copy-start.7
  357.9 75.5 %all-gather.32.cloned.1.call-start = ((), (), s32[]{:S(2)}) async-start(), calls=%async_computation.10 | async-start | bytes 2621440 | tf_op jit(solution)/shard_map/all_gather | solution.py:95
  388.9 129.3 %all-gather.34.cloned.1.call-start = ((), (), s32[]{:S(2)}) async-start(), calls=%async_computation.11 | async-start | bytes 2359296 | tf_op jit(solution)/shard_map/all_gather | solution.py:93
  490.1 75.5 %all-gather.36.cloned.1.call-start = ((), (), s32[]{:S(2)}) async-start(), calls=%async_computation.12 | async-start | bytes 2621440 | tf_op jit(solution)/shard_map/all_gather | solution.py:95
  521.1 129.9 %all-gather.38.cloned.1.call-start = ((), (), s32[]{:S(2)}) async-start(), calls=%async_computation.13 | async-start | bytes 2359296 | tf_op jit(solution)/shard_map/all_gather | solution.py:93
  591.0 5.5 copy-start.11
  622.9 75.4 %all-gather.40.cloned.1.call-start = ((), (), s32[]{:S(2)}) async-start(), calls=%async_computation.14 | async-start | bytes 2621440 | tf_op jit(solution)/shard_map/all_gather | solution.py:95
  653.9 129.3 %all-gather.42.cloned.1.call-start = ((), (), s32[]{:S(2)}) async-start(), calls=%async_computation.15 | async-start | bytes 2359296 | tf_op jit(solution)/shard_map/all_gather | solution.py:93
  755.2 75.5 %all-gather.44.cloned.1.call-start = ((), (), s32[]{:S(2)}) async-start(), calls=%async_computation.16 | async-start | bytes 2621440 | tf_op jit(solution)/shard_map/all_gather | solution.py:95
  786.1 129.7 %all-gather.46.cloned.1.call-start = ((), (), s32[]{:S(2)}) async-start(), calls=%async_computation.17 | async-start | bytes 2359296 | tf_op jit(solution)/shard_map/all_gather | solution.py:93
  856.0 5.5 copy-start.15
  887.7 75.4 %all-gather.48.cloned.1.call-start = ((), (), s32[]{:S(2)}) async-start(), calls=%async_computation.18 | async-start | bytes 2621440 | tf_op jit(solution)/shard_map/all_gather | solution.py:95
  918.7 128.9 %all-gather.50.cloned.1.call-start = ((), (), s32[]{:S(2)}) async-start(), calls=%async_computation.19 | async-start | bytes 2359296 | tf_op jit(solution)/shard_map/all_gather | solution.py:93
  1019.5 191.1 %all-gather.54.cloned.1.call-start = ((), (), s32[]{:S(2)}) async-start(), calls=%async_computation.21 | async-start | bytes 37748736 | tf_op jit(solution)/shard_map/all_gather | solution.py:15
  1024.3 232.1 %all-gather.52.cloned.1.call-start = ((), (), s32[]{:S(2)}) async-start(), calls=%async_computation.20 | async-start | bytes 2621440 | tf_op jit(solution)/shard_map/all_gather | solution.py:95
  1050.5 536.0 %all-gather.20.cloned.1.call-start = ((), (), s32[]{:S(2)}) async-start(), calls=%async_computation.4 | async-start | bytes 20971520 | tf_op jit(solution)/shard_map/all_gather | solution.py:15
  1282.6 5.9 copy-start.19
  1420.2 29.3 %all-to-all-start.3 = ((f32[8,1,64,1024]{3,2,1,0:T(8,128)}), f32[8,1,64,1024]{3,2,1,0:T(8,128)S(1)}, u32[]{:S(2)}, u32[]{:S(2)}) async-start(f32[8,1,64,1024]{3,2,1,0:T(8,128)} %bitcast.717), calls=%async_computation.3 | async-start | bytes 4194304 | tf_op jit(solution)/shard_map/all_to_all | solution.py:107
  1597.9 5.8 copy-start.36
  1618.5 15.2 slice-start
  1624.7 9.0 slice-start.1
  1645.0 5.6 copy-start.3
  1645.0 8.4 slice-start.2
  1645.0 8.4 slice-start.4
  1665.3 7.0 copy-start.53
  (93 other events, 216.3 us)
Sparse Core Ops, SparseCore 0:
  93.5 27.2 all-gather.21
  123.9 44.3 all-gather.23
  225.4 27.8 all-gather.25
  256.3 44.3 all-gather.27
  358.0 27.8 all-gather.29
  389.0 44.3 all-gather.31
  490.2 27.8 all-gather.33
  521.2 44.3 all-gather.35
  623.0 27.8 all-gather.37
  654.0 44.3 all-gather.39
  755.3 27.8 all-gather.41
  786.2 44.3 all-gather.43
  887.9 27.8 all-gather.45
  918.8 44.3 all-gather.47
  1019.7 27.9 all-gather.49
  1049.9 160.6 all-gather.53
  1212.0 44.3 all-gather.51
  1257.8 328.6 all-gather.19
